TPU v7x, 32 devices: a whole 2x2x4 slice. The times are simulated.
32 devices in a mesh: row: 16 (over z, x, core), col: 2 (over y).
Axes of the slice: x: 2, y: 2, z: 4, core: 2. Of those that a mesh axis runs over, the one named last changes fastest.
Arguments:
- seq_state: bfloat16 [1024, 1024], P('row'), may hold values from -6 to 6
- pair_state: bfloat16 [1024, 1024, 128], P('row', 'col'), may hold values from -8 to 8
- w_bias: bfloat16 [128, 32], replicated, may hold values from -12 to 12
- w_qkv: bfloat16 [3, 1024, 1024], P(None, None, 'col'), may hold values from -0.1875 to 0.1875
- w_gate: bfloat16 [1024, 1024], P(None, 'col'), may hold values from -0.1875 to 0.1875
- w_out: bfloat16 [1024, 1024], replicated, may hold values from -0.8984375 to 0.8984375
- w_seq_pair: bfloat16 [1024, 128], replicated, may hold values from -0.1875 to 0.1875
- w_pair_out: bfloat16 [128, 128], replicated, may hold values from -0.5 to 0.5
- w_up: bfloat16 [128, 512], replicated, may hold values from -0.5 to 0.5
- w_down: bfloat16 [512, 128], replicated, may hold values from -0.25 to 0.25
Outputs:
- seq_out: bfloat16 [1024, 1024], P('row')
- pair_out: bfloat16 [1024, 1024, 128], P('row', 'col')
All inputs are finite; a program needn't handle non-finite values.
Results may differ from a plain program's by a relative error of at most 0.018.
The roundings to bfloat16 on the way count: a program that leaves them out, or rounds other values in their place, can miss the bound.
Values may be sent and summed in bfloat16 or wider, within the bound.
A program may use at most 64 MiB of HBM per device.

v0:
```python
import functools
import math

import jax
import jax.numpy as jnp
from jax import lax
from jax.experimental import pallas as pl
from jax.experimental.pallas import tpu as pltpu
from jax.sharding import PartitionSpec as P

EPSILON = 1e-05
F32 = jnp.float32
BF16 = jnp.bfloat16
NN = (((1,), (0,)), ((), ()))
NT = (((1,), (1,)), ((), ()))
MESH = pl.DeviceIdType.MESH


def mm(a, b, dims=NN):
    return lax.dot_general(a, b, dims, preferred_element_type=F32)


def layer_norm(values):
    centred = values - jnp.mean(values, axis=-1, keepdims=True)
    variance = jnp.mean(centred * centred, axis=-1, keepdims=True)
    return centred * lax.rsqrt(variance + EPSILON)


def project_kernel(seq_ref, qkv_ref, gate_w_ref, q_ref, kv_ref, gate_ref, normed_ref):
    @pl.when(pl.program_id(0) == 0)
    def _():
        normed_ref[...] = layer_norm(seq_ref[...].astype(F32)).astype(BF16)

    normed = normed_ref[...]
    q_ref[...] = mm(normed, qkv_ref[0]).astype(BF16)
    kv_ref[0] = mm(normed, qkv_ref[1]).astype(BF16)
    kv_ref[1] = mm(normed, qkv_ref[2]).astype(BF16)
    gates = mm(normed, gate_w_ref[...])
    gate_ref[...] = 1.0 / (1.0 + jnp.exp(-gates))


def project(seq_state, w_qkv, w_gate):
    rows, depth = seq_state.shape
    width = w_gate.shape[1]
    tile = min(width, 128)
    return pl.pallas_call(
        project_kernel,
        grid=(width // tile,),
        in_specs=[
            pl.BlockSpec((rows, depth), lambda g: (0, 0)),
            pl.BlockSpec((3, depth, tile), lambda g: (0, 0, g)),
            pl.BlockSpec((depth, tile), lambda g: (0, g)),
        ],
        out_specs=[
            pl.BlockSpec((rows, tile), lambda g: (0, g)),
            pl.BlockSpec((2, rows, tile), lambda g: (0, 0, g)),
            pl.BlockSpec((rows, tile), lambda g: (0, g)),
        ],
        out_shape=[
            jax.ShapeDtypeStruct((rows, width), BF16),
            jax.ShapeDtypeStruct((2, rows, width), BF16),
            jax.ShapeDtypeStruct((rows, width), F32),
        ],
        scratch_shapes=[pltpu.VMEM((rows, depth), BF16)],
        compiler_params=pltpu.CompilerParams(vmem_limit_bytes=60 << 20),
        name="project",
    )(seq_state, w_qkv, w_gate)


def greet(row_count, groups):
    row, col = lax.axis_index("row"), lax.axis_index("col")
    barrier = pltpu.get_barrier_semaphore()
    for d in range(1, row_count):
        pl.semaphore_signal(
            barrier, inc=1, device_id={"row": lax.rem(row + d, row_count)}, device_id_type=MESH
        )
    for d in range(1, groups):
        pl.semaphore_signal(
            barrier, inc=1, device_id={"col": lax.rem(col + d, groups)}, device_id_type=MESH
        )
    pl.semaphore_wait(barrier, row_count + groups - 2)


def split_rows(row_count):
    core = 2 if row_count % 2 == 0 else 1
    near = 2 if (row_count // core) % 2 == 0 else 1
    return row_count // core // near, near, core


def centre_matrix(channels):
    shape = (channels, channels)
    same = lax.broadcasted_iota(jnp.int32, shape, 0) == lax.broadcasted_iota(jnp.int32, shape, 1)
    return jnp.where(same, 1.0, 0.0) - 1.0 / channels


def bias_kernel(
    row_count, groups, pair_ref, w_ref, kv_ref,
    own_ref, kv_all_ref, *rest
):
    received = rest[: groups - 1]
    (send_buf, kv_send, kv_recv, kv_local, bias_send, bias_recv) = rest[groups - 1 :]
    step, steps = pl.program_id(0), pl.num_programs(0)
    step_rows, local_heads, cols = own_ref.shape
    row, col = lax.axis_index("row"), lax.axis_index("col")
    far_n, near_n, core_n = split_rows(row_count)
    far, near, core = row // (near_n * core_n), (row // core_n) % near_n, row % core_n

    def index(f, n, c):
        return (lax.rem(f, far_n) * near_n + lax.rem(n, near_n)) * core_n + lax.rem(c, core_n)

    def kv_copy(slot, source, block, target):
        return pltpu.make_async_remote_copy(
            src_ref=source,
            dst_ref=kv_all_ref.at[block],
            send_sem=kv_send.at[slot],
            recv_sem=kv_recv.at[block],
            device_id={"row": target},
            device_id_type=MESH,
        )

    def far_copies():
        return [
            kv_copy(d - 1, kv_ref, row, index(far + d, near, core)) for d in range(1, far_n)
        ]

    def near_copies(first, last):
        out = []
        for e in range(1, near_n):
            for d in range(first, last):
                block = index(far + d, near, core)
                source = kv_ref if d == 0 else kv_all_ref.at[block]
                slot = far_n - 1 + (e - 1) * far_n + d
                out.append(kv_copy(slot, source, block, index(far, near + e, core)))
        return out

    def core_copies(first_near, last_near, first, last):
        out = []
        for c in range(1, core_n):
            for e in range(first_near, last_near):
                for d in range(first, last):
                    block = index(far + d, near + e, core)
                    source = kv_ref if d == 0 and e == 0 else kv_all_ref.at[block]
                    slot = near_n * far_n - 1 + ((c - 1) * near_n + e) * far_n + d
                    out.append(kv_copy(slot, source, block, index(far, near, core + c)))
        return out

    def wait_block(block):
        kv_copy(0, kv_ref, block, row).wait_recv()

    def local_copy():
        return pltpu.make_async_copy(kv_ref, kv_all_ref.at[row], kv_local)

    def bias_copy(s, at):
        return pltpu.make_async_remote_copy(
            src_ref=send_buf.at[lax.rem(at, 2), s - 1],
            dst_ref=received[s - 1].at[pl.ds(at * step_rows, step_rows)],
            send_sem=bias_send.at[lax.rem(at, 2), s - 1],
            recv_sem=bias_recv.at[at, s - 1],
            device_id={"col": lax.rem(col + s, groups)},
            device_id_type=MESH,
        )

    @pl.when(step == 0)
    def _():
        greet(row_count, groups)
        for copy in far_copies() + near_copies(0, 1) + core_copies(0, 1, 0, 1):
            copy.start()
        local_copy().start()

    @pl.when(step >= 1)
    def _():
        for s in range(1, groups):
            bias_copy(s, step - 1).start()

    @pl.when(step >= 2)
    def _():
        for s in range(1, groups):
            bias_copy(s, step - 2).wait_send()

    slot = lax.rem(step, 2)
    w_rows = jnp.concatenate(
        [w_ref[lax.rem(col + s, groups)].astype(F32) for s in range(groups)], axis=0
    ).astype(BF16)
    centre = centre_matrix(pair_ref.shape[2]).astype(BF16)
    for r in range(step_rows):
        centred = mm(pair_ref[r], centre)
        variance = jnp.mean(centred * centred, axis=-1, keepdims=True)
        normed = (centred * lax.rsqrt(variance + EPSILON)).astype(BF16)
        bias = mm(w_rows, normed, NT).astype(BF16)
        own_ref[r] = bias[:local_heads]
        for s in range(1, groups):
            send_buf[slot, s - 1, r] = bias[s * local_heads : (s + 1) * local_heads]

    @pl.when(step == steps - 1)
    def _():
        for s in range(1, groups):
            bias_copy(s, step).start()
        for d in range(1, far_n):
            wait_block(index(far + d, near, core))
            for copy in near_copies(d, d + 1) + core_copies(0, 1, d, d + 1):
                copy.start()
        for e in range(1, near_n):
            for d in range(far_n):
                wait_block(index(far + d, near + e, core))
                for copy in core_copies(e, e + 1, d, d + 1):
                    copy.start()
        for c in range(1, core_n):
            for e in range(near_n):
                for d in range(far_n):
                    wait_block(index(far + d, near + e, core + c))
        local_copy().wait()
        for copy in far_copies() + near_copies(0, far_n) + core_copies(0, near_n, 0, far_n):
            copy.wait_send()
        for s in range(1, groups):
            @pl.when(step >= 1)
            def _():
                bias_copy(s, step - 1).wait_send()

            bias_copy(s, step).wait_send()

            @pl.loop(0, steps)
            def _(at):
                bias_copy(s, at).wait_recv()


def bias_and_gather(pair_state, w_rows, kv_local, row_count, groups, step_rows):
    rows, cols, channels = pair_state.shape
    local_heads = w_rows.shape[1]
    steps = rows // step_rows
    whole = lambda x: pl.BlockSpec(x.shape, lambda g: (0,) * x.ndim)
    anywhere = pl.BlockSpec(memory_space=pl.ANY)
    part = jax.ShapeDtypeStruct((rows, local_heads, cols), BF16)
    out = pl.pallas_call(
        functools.partial(bias_kernel, row_count, groups),
        grid=(steps,),
        in_specs=[
            pl.BlockSpec((step_rows, cols, channels), lambda g: (g, 0, 0)),
            whole(w_rows),
            anywhere,
        ],
        out_specs=[
            pl.BlockSpec((step_rows, local_heads, cols), lambda g: (g, 0, 0)),
            anywhere,
        ]
        + [anywhere] * (groups - 1),
        out_shape=[part, jax.ShapeDtypeStruct((row_count,) + kv_local.shape, BF16)]
        + [part] * (groups - 1),
        scratch_shapes=[
            pltpu.VMEM((2, max(1, groups - 1), step_rows, local_heads, cols), BF16),
            pltpu.SemaphoreType.DMA((row_count,)),
            pltpu.SemaphoreType.DMA((row_count,)),
            pltpu.SemaphoreType.DMA,
            pltpu.SemaphoreType.DMA((2, max(1, groups - 1))),
            pltpu.SemaphoreType.DMA((steps, max(1, groups - 1))),
        ],
        compiler_params=pltpu.CompilerParams(
            vmem_limit_bytes=60 << 20, collective_id=0, has_side_effects=True
        ),
        name="bias_gather",
    )(pair_state, w_rows, kv_local)
    return out[1], [out[0]] + list(out[2:])


def mix_chunk(head_size, groups, col, q, k_ref, v_ref, gates, bias_refs):
    rows, heads, cols = bias_refs[0].shape
    width = q.shape[1]
    lane_head = lax.broadcasted_iota(jnp.int32, (heads, width), 1) // head_size
    own = (lane_head == lax.broadcasted_iota(jnp.int32, (heads, width), 0)).astype(F32)
    scale = 1.0 / math.sqrt(head_size)
    blocks = cols // k_ref.shape[1]
    queries = (q.astype(F32)[:, None, :] * own[None]).reshape(rows * heads, width).astype(BF16)
    scores, parts = [], []
    for s in range(groups):
        start = lax.rem(col + (groups - s), groups) * blocks
        parts.append(start)
        keys = k_ref[pl.ds(start, blocks)].reshape(cols, width)
        scores.append(
            mm(queries, keys, NT) * scale
            + bias_refs[s][...].astype(F32).reshape(rows * heads, cols)
        )
    peak = functools.reduce(jnp.maximum, [jnp.max(x, axis=-1, keepdims=True) for x in scores])
    weights = [jnp.exp(x - peak) for x in scores]
    inverse = 1.0 / sum(jnp.sum(x, axis=-1, keepdims=True) for x in weights)
    mixed = sum(
        mm((x * inverse).astype(BF16), v_ref[pl.ds(start, blocks)].reshape(cols, width))
        for x, start in zip(weights, parts)
    )
    mixed = jnp.sum(mixed.reshape(rows, heads, width) * own[None], axis=1)
    return (mixed * gates).astype(BF16)


def attend_kernel(
    head_size, row_count, groups, q_ref, k_ref, v_ref, gate_ref, seq_ref, w_out_ref,
    w_sides_ref, *rest
):
    bias_refs = rest[:groups]
    (seq_out_ref, left_ref, right_all_ref) = rest[groups : groups + 3]
    (attended, projected, mix_send, mix_recv, side_send, side_recv, side_local) = rest[groups + 3 :]
    step, steps = pl.program_id(0), pl.num_programs(0)
    chunk, width = q_ref.shape
    rows, depth = seq_ref.shape
    row, col = lax.axis_index("row"), lax.axis_index("col")
    blocks = right_all_ref.shape[0]

    def mix_copy(s, at):
        here = pl.ds(at * chunk, chunk)
        return pltpu.make_async_remote_copy(
            src_ref=attended.at[0, here],
            dst_ref=attended.at[s, here],
            send_sem=mix_send.at[at, s],
            recv_sem=mix_recv.at[at, s],
            device_id={"col": lax.rem(col + s, groups)},
            device_id_type=MESH,
        )

    def side_copy(d):
        return pltpu.make_async_remote_copy(
            src_ref=projected,
            dst_ref=right_all_ref.at[lax.rem(row, blocks)],
            send_sem=side_send.at[d],
            recv_sem=side_recv.at[lax.rem(row, blocks)],
            device_id={"row": lax.rem(row + d, row_count)},
            device_id_type=MESH,
        )

    def side_wait(block):
        pltpu.make_async_remote_copy(
            src_ref=projected,
            dst_ref=right_all_ref.at[block],
            send_sem=side_send.at[0],
            recv_sem=side_recv.at[block],
            device_id={"row": row},
            device_id_type=MESH,
        ).wait_recv()

    @pl.when(step == 0)
    def _():
        greet(row_count, groups)

    @pl.when(step >= 1)
    def _():
        for s in range(1, groups):
            mix_copy(s, step - 1).start()

    attended[0, pl.ds(step * chunk, chunk)] = mix_chunk(
        head_size, groups, col, q_ref[...], k_ref, v_ref, gate_ref[...], bias_refs
    )

    @pl.when(step == steps - 1)
    def _():
        total = seq_ref[...].astype(F32)
        for s in range(1, groups):
            mix_copy(s, step).start()
        start = pl.multiple_of(col * width, width)
        update = mm(attended[0], w_out_ref[pl.ds(start, width), :])
        for s in range(1, groups):
            for at in range(steps_static(rows, chunk)):
                mix_copy(s, at).wait_recv()
            source = lax.rem(col + (groups - s), groups)
            start = pl.multiple_of(source * width, width)
            update += mm(attended[s], w_out_ref[pl.ds(start, width), :])
        seq_out = (total + update).astype(BF16)
        seq_out_ref[...] = seq_out
        normed = layer_norm(seq_out.astype(F32)).astype(BF16)
        sides = mm(normed, w_sides_ref[...])
        inner = sides.shape[1] // 2
        lanes = lax.broadcasted_iota(jnp.int32, sides.shape, 1)
        projected[...] = jnp.where(lanes < inner, pltpu.roll(sides, inner, 1), sides).astype(BF16)
        mine = row // blocks == col

        @pl.when(mine)
        def _():
            for d in range(1, row_count):
                side_copy(d).start()
            pltpu.make_async_copy(
                projected, right_all_ref.at[lax.rem(row, blocks)], side_local
            ).start()

        left_ref[...] = jnp.where(lanes < inner, sides.astype(BF16).astype(F32), 1.0)

        for b in range(blocks):
            @pl.when(col * blocks + b != row)
            def _():
                side_wait(b)

        @pl.when(mine)
        def _():
            pltpu.make_async_copy(
                projected, right_all_ref.at[lax.rem(row, blocks)], side_local
            ).wait()
            for d in range(1, row_count):
                side_copy(d).wait_send()

        for s in range(1, groups):
            for at in range(steps_static(rows, chunk)):
                mix_copy(s, at).wait_send()


def steps_static(rows, chunk):
    return rows // chunk


def attend(queries, kv_all, gates, biases, seq_state, w_out, w_seq_pair, head_size, row_count, chunk):
    rows, depth = seq_state.shape
    groups = len(biases)
    heads, cols = biases[0].shape[1:]
    width = queries.shape[1]
    inner = w_seq_pair.shape[1] // 2
    blocks = cols // rows
    whole = lambda x: pl.BlockSpec(x.shape, lambda g: (0,) * x.ndim, pipeline_mode=pl.Buffered(1))
    side = lambda i: pl.BlockSpec(
        (row_count, None, rows, width), lambda g: (0, i, 0, 0), pipeline_mode=pl.Buffered(1)
    )
    steps = rows // chunk
    fixed = lambda shape: pl.BlockSpec(shape, lambda g: (0,) * len(shape))
    return pl.pallas_call(
        functools.partial(attend_kernel, head_size, row_count, groups),
        grid=(steps,),
        in_specs=[
            pl.BlockSpec((chunk, width), lambda g: (g, 0)),
            side(0),
            side(1),
            pl.BlockSpec((chunk, width), lambda g: (g, 0)),
            whole(seq_state),
            whole(w_out),
            whole(w_seq_pair),
        ]
        + [pl.BlockSpec((chunk, heads, cols), lambda g: (g, 0, 0))] * groups,
        out_specs=[
            fixed((rows, depth)),
            fixed((rows, 2 * inner)),
            pl.BlockSpec(memory_space=pl.ANY),
        ],
        out_shape=[
            jax.ShapeDtypeStruct((rows, depth), BF16),
            jax.ShapeDtypeStruct((rows, 2 * inner), F32),
            jax.ShapeDtypeStruct((blocks, rows, 2 * inner), BF16),
        ],
        scratch_shapes=[
            pltpu.VMEM((groups, rows, width), BF16),
            pltpu.VMEM((rows, 2 * inner), BF16),
            pltpu.SemaphoreType.DMA((steps, groups)),
            pltpu.SemaphoreType.DMA((steps, groups)),
            pltpu.SemaphoreType.DMA((row_count,)),
            pltpu.SemaphoreType.DMA((blocks,)),
            pltpu.SemaphoreType.DMA,
        ],
        compiler_params=pltpu.CompilerParams(
            vmem_limit_bytes=60 << 20, collective_id=1, has_side_effects=True
        ),
        name="attend",
    )(queries, kv_all, kv_all, gates, seq_state, w_out, w_seq_pair, *biases)


def pair_kernel(
    left_ref, pair_ref, right_ref, w_pair_ref, up_ref, down_ref, out_ref, weights_ref, shift_ref
):
    step_rows, cols, channels = pair_ref.shape
    base = pl.program_id(0) * step_rows

    @pl.when(pl.program_id(0) == 0)
    def _():
        inner = w_pair_ref.shape[0] // 2
        centre = centre_matrix(channels)
        eye = centre + 1.0 / channels
        both = jnp.concatenate(
            [mm(w_pair_ref[...], centre.astype(BF16)), w_pair_ref[...].astype(F32)], axis=1
        ).astype(BF16)
        top = jnp.concatenate([centre, eye], axis=1).astype(BF16)
        weights_ref[...] = jnp.concatenate([top, both[:inner], -both[inner:]], axis=0)
        shift_ref[...] = mm(left_ref[:, :inner].astype(BF16), both[inner:])

    right = right_ref[...].astype(F32)
    weights = weights_ref[...]
    for r in range(step_rows):
        sides = (right * left_ref[pl.ds(base + r, 1), :]).astype(BF16)
        both = mm(jnp.concatenate([pair_ref[r], sides], axis=1), weights)
        both += shift_ref[pl.ds(base + r, 1), :]
        centred, updated = both[:, :channels], both[:, channels:]
        variance = jnp.mean(centred * centred, axis=-1, keepdims=True)
        normed = (centred * lax.rsqrt(variance + EPSILON)).astype(BF16)
        hidden = jnp.maximum(mm(normed, up_ref[...]), 0.0).astype(BF16)
        out_ref[r] = (updated + mm(hidden, down_ref[...])).astype(BF16)


def pair_update(pair_state, left, right, w_pair_out, w_up, w_down, step_rows):
    rows, cols, channels = pair_state.shape
    whole = lambda x: pl.BlockSpec(x.shape, lambda g: (0,) * x.ndim)
    return pl.pallas_call(
        pair_kernel,
        grid=(rows // step_rows,),
        in_specs=[
            whole(left),
            pl.BlockSpec((step_rows, cols, channels), lambda g: (g, 0, 0)),
            whole(right),
            whole(w_pair_out),
            whole(w_up),
            whole(w_down),
        ],
        out_specs=pl.BlockSpec((step_rows, cols, channels), lambda g: (g, 0, 0)),
        out_shape=jax.ShapeDtypeStruct(pair_state.shape, BF16),
        scratch_shapes=[
            pltpu.VMEM((2 * channels, 2 * channels), BF16),
            pltpu.VMEM((rows, 2 * channels), F32),
        ],
        compiler_params=pltpu.CompilerParams(vmem_limit_bytes=60 << 20),
        name="pair_update",
    )(left, pair_state, right, w_pair_out, w_up, w_down)


def body(row_count, groups, seq_state, pair_state, w_bias, w_qkv, w_gate, w_out, w_seq_pair, w_pair_out, w_up, w_down):
    rows_here, model_width = seq_state.shape
    cols_here, channels = pair_state.shape[1:]
    head_count = w_bias.shape[1]
    local_width = w_gate.shape[1]
    head_size = model_width // head_count
    local_heads = local_width // head_size
    queries, kv_local, gates = project(seq_state, w_qkv, w_gate)
    w_rows = w_bias.T.reshape(groups, local_heads, channels)
    kv_all, biases = bias_and_gather(
        pair_state, w_rows, kv_local, row_count, groups, math.gcd(rows_here, 8)
    )
    seq_out, left, right = attend(
        queries, kv_all, gates, biases, seq_state, w_out, w_seq_pair,
        head_size, row_count, math.gcd(rows_here, 32),
    )
    right = right.reshape(cols_here, right.shape[-1])
    pair_out = pair_update(pair_state, left, right, w_pair_out, w_up, w_down, math.gcd(rows_here, 16))
    return seq_out, pair_out


def solution(mesh):
    return jax.shard_map(
        functools.partial(body, mesh.shape["row"], mesh.shape["col"]),
        mesh=mesh,
        in_specs=(
            P("row", None),
            P("row", "col", None),
            P(),
            P(None, None, "col"),
            P(None, "col"),
            P(),
            P(),
            P(),
            P(),
            P(),
        ),
        out_specs=(P("row", None), P("row", "col", None)),
        check_vma=False,
    )
```

profile of v0, /device:TPU:7, one launch (start us, length us, event | category | flops | bytes accessed | tf_op | source)
XLA Modules:
  0.0 91.7 jit_solution(2793845778939760690)
XLA Ops:
  0.6 4.6 %project.1 = (bf16[64,512]{1,0:T(8,128)(2,1)}, bf16[2,64,512]{2,1,0:T(8,128)(2,1)}, f32[64,512]{1,0:T(8,128)}) custom-call(bf16[64,1024]{1,0:T(8,128)(2,1)} %seq_ref.3, bf16[3,1024,512]{2,1,0:T(8,128)(2,1)} %qkv_ref.1, bf16[1024,512]{1,0:T(8,128)(2,1)} %gate_w_ref.1), custom_call_target="tpu_custom_call" | custom-call | tf_op jit(solution)/shard_map/project/pallas_call | solution.py:46
  5.2 37.6 %bias_gather.1 = (bf16[64,16,512]{2,1,0:T(8,128)(2,1)}, bf16[16,2,64,512]{3,2,1,0:T(8,128)(2,1)}, bf16[64,16,512]{2,1,0:T(8,128)(2,1)}) custom-call(bf16[64,512,128]{2,1,0:T(8,128)(2,1)} %pair_ref.3, bf16[2,16,128]{2,1,0:T(8,128)(2,1)} %bitcast.5, bf16[2,64,512]{2,1,0:T(8,128)(2,1)} %get-tuple-element.12.kv_ref), custom_call_target="tpu_custom_call" | custom-call | tf_op jit(solution)/shard_map/bias_gather/pallas_call | solution.py:233
  42.9 19.0 %attend.1 = (bf16[64,1024]{1,0:T(8,128)(2,1)}, f32[64,128]{1,0:T(8,128)}, bf16[8,64,128]{2,1,0:T(8,128)(2,1)}) custom-call(bf16[64,512]{1,0:T(8,128)(2,1)} %get-tuple-element.11.q_ref, bf16[16,2,64,512]{3,2,1,0:T(8,128)(2,1)} %get-tuple-element.13.k_ref.v_ref, bf16[16,2,64,512]{3,2,1,0:T(8,128)(2,1)} %get-tuple-element.13.k_ref.v_ref, ...), custom_call_target="tpu_custom_call" | custom-call | tf_op jit(solution)/shard_map/attend/pallas_call | solution.py:416
  61.9 0.0 copy-start
  61.9 29.1 %pair_update.1 = bf16[64,512,128]{2,1,0:T(8,128)(2,1)} custom-call(f32[64,128]{1,0:T(8,128)} %get-tuple-element.18.left_ref, bf16[64,512,128]{2,1,0:T(8,128)(2,1)} %pair_ref.3, bf16[512,128]{1,0:T(8,128)(2,1)} %bitcast.4, bf16[128,128]{1,0:T(8,128)(2,1)} %w_pair_ref.1, bf16[128,512]{1,0:T(8,128)(2,1)} %up_ref.1, bf16[512,128]{1,0:T(8,128)(2,1)} %down_ref.1), custom_call_target="tpu_custom_call" | custom-call | tf_op jit(solution)/shard_map/pair_update/pallas_call | solution.py:489
  91.0 0.0 copy-done
  91.0 0.7 copy.13
Async XLA Ops:
  61.9 29.1 %copy-start = (bf16[64,1024]{1,0:T(8,128)(2,1)S(1)}, bf16[64,1024]{1,0:T(8,128)(2,1)}, u32[]{:S(2)}) copy-start(bf16[64,1024]{1,0:T(8,128)(2,1)} %get-tuple-element.22) | copy-start | bytes 393220
where the time goes:
time: 91.9 us; the launch traced here: 91.7 us
  Pallas kernels  90.4 us (98%)
    pallas_call x1, Pallas kernels, bias_and_gather(): pl.pallas_call(functools.partial(bias_kernel, row_count, groups), grid=(s...  37.6 us
    pallas_call x1, Pallas kernels, pair_update(): pl.pallas_call(pair_kernel, grid=(rows // step_rows,), in_specs=[whole(le...  29.1 us
    pallas_call x1, Pallas kernels, attend(): pl.pallas_call(functools.partial(attend_kernel, head_size, row_count, gro...  19 us
    pallas_call x1, Pallas kernels, project(): pl.pallas_call(project_kernel, grid=(width // tile,), in_specs=[pl.BlockS...  4.61 us

commit v1 on v0

--- a/solution.py
+++ b/solution.py
@@ -453,34 +453,53 @@
 
 
 def pair_kernel(
-    left_ref, pair_ref, right_ref, w_pair_ref, up_ref, down_ref, out_ref, weights_ref, shift_ref
+    left_ref, pair_ref, right_ref, w_pair_ref, up_ref, down_ref, out_ref,
+    w_pair_t, up_t, down_t, right_t, left_t, updated_buf, centred_buf, scale_buf, hidden_buf,
 ):
     step_rows, cols, channels = pair_ref.shape
+    inner = w_pair_ref.shape[0] // 2
     base = pl.program_id(0) * step_rows
 
     @pl.when(pl.program_id(0) == 0)
     def _():
-        inner = w_pair_ref.shape[0] // 2
-        centre = centre_matrix(channels)
-        eye = centre + 1.0 / channels
-        both = jnp.concatenate(
-            [mm(w_pair_ref[...], centre.astype(BF16)), w_pair_ref[...].astype(F32)], axis=1
-        ).astype(BF16)
-        top = jnp.concatenate([centre, eye], axis=1).astype(BF16)
-        weights_ref[...] = jnp.concatenate([top, both[:inner], -both[inner:]], axis=0)
-        shift_ref[...] = mm(left_ref[:, :inner].astype(BF16), both[inner:])
-
-    right = right_ref[...].astype(F32)
-    weights = weights_ref[...]
-    for r in range(step_rows):
-        sides = (right * left_ref[pl.ds(base + r, 1), :]).astype(BF16)
-        both = mm(jnp.concatenate([pair_ref[r], sides], axis=1), weights)
-        both += shift_ref[pl.ds(base + r, 1), :]
-        centred, updated = both[:, :channels], both[:, channels:]
-        variance = jnp.mean(centred * centred, axis=-1, keepdims=True)
-        normed = (centred * lax.rsqrt(variance + EPSILON)).astype(BF16)
-        hidden = jnp.maximum(mm(normed, up_ref[...]), 0.0).astype(BF16)
-        out_ref[r] = (updated + mm(hidden, down_ref[...])).astype(BF16)
+        w_pair_t[...] = w_pair_ref[...].T
+        up_t[...] = up_ref[...].T
+        down_t[...] = down_ref[...].T
+        right_t[...] = right_ref[...].T[:inner]
+        left = left_ref[:, :inner]
+        rows = left.shape[0]
+        padded = jnp.concatenate([left, jnp.zeros((left_t.shape[1] - rows, inner), F32)], axis=0)
+        left_t[...] = padded.T
+
+    lefts = pltpu.roll(left_t[...], lax.rem(left_t.shape[1] - base, left_t.shape[1]), 1)
+    right = right_t[...]
+
+    def features(r):
+        slot = r % 3
+        left = lefts[:, r : r + 1].astype(BF16)
+        sides = jnp.concatenate([left * right, left - right], axis=0)
+        updated = pair_ref[r].T.astype(F32) + mm(w_pair_t[...], sides)
+        centred = updated - jnp.mean(updated, axis=0, keepdims=True)
+        variance = jnp.mean(centred * centred, axis=0, keepdims=True)
+        updated_buf[slot] = updated
+        centred_buf[r % 2] = centred.astype(BF16)
+        scale_buf[slot] = lax.rsqrt(variance + EPSILON)
+
+    def expand(r):
+        hidden_buf[r % 2] = jnp.maximum(mm(up_t[...], centred_buf[r % 2]).astype(BF16), 0.0)
+
+    def contract(r):
+        slot = r % 3
+        change = mm(down_t[...], hidden_buf[r % 2]) * scale_buf[slot]
+        out_ref[r] = (updated_buf[slot] + change).astype(BF16).T
+
+    for t in range(step_rows + 2):
+        if t < step_rows:
+            features(t)
+        if 0 <= t - 1 < step_rows:
+            expand(t - 1)
+        if t >= 2:
+            contract(t - 2)
 
 
 def pair_update(pair_state, left, right, w_pair_out, w_up, w_down, step_rows):
@@ -500,8 +519,15 @@
         out_specs=pl.BlockSpec((step_rows, cols, channels), lambda g: (g, 0, 0)),
         out_shape=jax.ShapeDtypeStruct(pair_state.shape, BF16),
         scratch_shapes=[
-            pltpu.VMEM((2 * channels, 2 * channels), BF16),
-            pltpu.VMEM((rows, 2 * channels), F32),
+            pltpu.VMEM(w_pair_out.shape[::-1], BF16),
+            pltpu.VMEM(w_up.shape[::-1], BF16),
+            pltpu.VMEM(w_down.shape[::-1], BF16),
+            pltpu.VMEM((right.shape[1] // 2, cols), BF16),
+            pltpu.VMEM((right.shape[1] // 2, max(128, rows)), F32),
+            pltpu.VMEM((3, channels, cols), F32),
+            pltpu.VMEM((2, channels, cols), BF16),
+            pltpu.VMEM((3, 1, cols), F32),
+            pltpu.VMEM((2, w_up.shape[1], cols), BF16),
         ],
         compiler_params=pltpu.CompilerParams(vmem_limit_bytes=60 << 20),
         name="pair_update",

time: 91.9 us -> 85.6 us (0.931)
  Pallas kernels: 90.4 us -> 84 us
    pallas_call x1, Pallas kernels: 29.1 us -> 22.8 us  [pair_update(): pl.pallas_call(pair_kernel, grid=(rows // step_rows,), in_specs=[whole(le...]
where the time goes in v1:
time: 85.6 us; the launch traced here: 85.3 us
  Pallas kernels  84 us (98%)
    pallas_call x1, Pallas kernels, bias_and_gather(): pl.pallas_call(functools.partial(bias_kernel, row_count, groups), grid=(s...  37.6 us
    pallas_call x1, Pallas kernels, pair_update(): pl.pallas_call(pair_kernel, grid=(rows // step_rows,), in_specs=[whole(le...  22.8 us
    pallas_call x1, Pallas kernels, attend(): pl.pallas_call(functools.partial(attend_kernel, head_size, row_count, gro...  19 us
    pallas_call x1, Pallas kernels, project(): pl.pallas_call(project_kernel, grid=(width // tile,), in_specs=[pl.BlockS...  4.61 us

profile of v1, /device:TPU:7, one launch (start us, length us, event | category | flops | bytes accessed | tf_op | source)
XLA Modules:
  0.0 85.3 jit_solution(2392207497331048039)
XLA Ops:
  0.6 4.6 %project.1 = (bf16[64,512]{1,0:T(8,128)(2,1)}, bf16[2,64,512]{2,1,0:T(8,128)(2,1)}, f32[64,512]{1,0:T(8,128)}) custom-call(bf16[64,1024]{1,0:T(8,128)(2,1)} %seq_ref.3, bf16[3,1024,512]{2,1,0:T(8,128)(2,1)} %qkv_ref.1, bf16[1024,512]{1,0:T(8,128)(2,1)} %gate_w_ref.1), custom_call_target="tpu_custom_call" | custom-call | tf_op jit(solution)/shard_map/project/pallas_call | solution.py:46
  5.2 37.6 %bias_gather.1 = (bf16[64,16,512]{2,1,0:T(8,128)(2,1)}, bf16[16,2,64,512]{3,2,1,0:T(8,128)(2,1)}, bf16[64,16,512]{2,1,0:T(8,128)(2,1)}) custom-call(bf16[64,512,128]{2,1,0:T(8,128)(2,1)} %pair_ref.3, bf16[2,16,128]{2,1,0:T(8,128)(2,1)} %bitcast.5, bf16[2,64,512]{2,1,0:T(8,128)(2,1)} %get-tuple-element.12.kv_ref), custom_call_target="tpu_custom_call" | custom-call | tf_op jit(solution)/shard_map/bias_gather/pallas_call | solution.py:233
  42.9 19.0 %attend.1 = (bf16[64,1024]{1,0:T(8,128)(2,1)}, f32[64,128]{1,0:T(8,128)}, bf16[8,64,128]{2,1,0:T(8,128)(2,1)}) custom-call(bf16[64,512]{1,0:T(8,128)(2,1)} %get-tuple-element.11.q_ref, bf16[16,2,64,512]{3,2,1,0:T(8,128)(2,1)} %get-tuple-element.13.k_ref.v_ref, bf16[16,2,64,512]{3,2,1,0:T(8,128)(2,1)} %get-tuple-element.13.k_ref.v_ref, ...), custom_call_target="tpu_custom_call" | custom-call | tf_op jit(solution)/shard_map/attend/pallas_call | solution.py:416
  61.9 0.0 copy-start
  61.9 22.8 %pair_update.1 = bf16[64,512,128]{2,1,0:T(8,128)(2,1)} custom-call(f32[64,128]{1,0:T(8,128)} %get-tuple-element.18.left_ref, bf16[64,512,128]{2,1,0:T(8,128)(2,1)} %pair_ref.3, bf16[512,128]{1,0:T(8,128)(2,1)} %bitcast.4, bf16[128,128]{1,0:T(8,128)(2,1)} %w_pair_ref.1, bf16[128,512]{1,0:T(8,128)(2,1)} %up_ref.1, bf16[512,128]{1,0:T(8,128)(2,1)} %down_ref.1), custom_call_target="tpu_custom_call" | custom-call | tf_op jit(solution)/shard_map/pair_update/pallas_call | solution.py:508
  84.7 0.0 copy-done
  84.7 0.7 copy.13
Async XLA Ops:
  61.9 22.8 %copy-start = (bf16[64,1024]{1,0:T(8,128)(2,1)S(1)}, bf16[64,1024]{1,0:T(8,128)(2,1)}, u32[]{:S(2)}) copy-start(bf16[64,1024]{1,0:T(8,128)(2,1)} %get-tuple-element.22) | copy-start | bytes 393220
